TPU v7x, 32 devices: a whole 2x2x4 slice. The times are simulated.
32 devices in a mesh: sub: 16 (over z, y, core), tm: 2 (over x).
Axes of the slice: x: 2, y: 2, z: 4, core: 2. Of those that a mesh axis runs over, the one named last changes fastest.
Arguments:
- voltages: bfloat16 [192, 2, 96, 2048], P('sub', None, None, 'tm'), may hold values from -6 to 6
- pointing_table: bfloat16 [192, 2, 320, 96], P('sub'), may hold values from -0.4375 to 0.4375
- beam_pointing: int32 [256], replicated, may hold values from 0 to 319
- subband_order: int32 [192], replicated, may hold values from 0 to 191, each once
- live_subbands: int32 [1], replicated, may hold values from 152 to 192
- filter_taps: float32 [16, 16], replicated, may hold values from -0.36 to 0.36
Outputs:
- synthesised: bfloat16 [256, 12, 2, 32768], P('sub', None, None, 'tm')
Inputs may be any that keep to these rules, and one draw needn't show every extreme that they name: `subband_order`: each slot is named by exactly one frequency.
All inputs are finite; a program needn't handle non-finite values.
Results may differ from a plain program's by a relative error of at most 0.0052.
Values may be sent and summed in bfloat16 or wider, within the bound.
No kernel may reach another device: no remote copies, remote signals or barrier semaphores. Data moves between devices by JAX's collectives and lax.ppermute only.
A program may use at most 192 MiB of HBM per device.

v0:
```python
import math

import jax
import jax.numpy as jnp
from jax import lax
from jax.sharding import PartitionSpec as P


def shifted(block, axis, distance):
    devices = range(lax.axis_size(axis))
    route = [(i - distance, i) for i in devices if i - distance in devices]
    return lax.ppermute(block, axis, route)


def inverse_table(channel_count):
    channel_index = jnp.arange(channel_count, dtype=jnp.int32)
    phase = (jnp.outer(channel_index, channel_index) % channel_count).astype(jnp.float32) * (
        2.0 * math.pi / channel_count
    )
    cosine = jnp.cos(phase).astype(jnp.bfloat16)
    sine_table = jnp.sin(phase).astype(jnp.bfloat16)
    upper_rows = jnp.stack([cosine, -sine_table], axis=1)
    lower_rows = jnp.stack([sine_table, cosine], axis=1)
    return jnp.stack([upper_rows, lower_rows], axis=0)


def spectrum_channels(beam_rows, subband_order, live_subbands, inverse_rows):
    slot_count = beam_rows.shape[0]
    channel_count = inverse_rows.shape[1]
    spectrum = jnp.take(beam_rows, subband_order, axis=0)
    live_mask = jnp.arange(slot_count, dtype=jnp.int32) < live_subbands[0]
    spectrum = jnp.where(live_mask[:, None, None, None], spectrum, jnp.zeros_like(spectrum))
    grouped = spectrum.reshape(
        slot_count // channel_count, channel_count, beam_rows.shape[1], 2, beam_rows.shape[3]
    )
    channels = jnp.einsum(
        "qkpc,gcbpt->bgqkt", inverse_rows, grouped, preferred_element_type=jnp.float32
    )
    return (grouped, channels)


def polyphase(channels, earlier, filter_taps):
    length = channels.shape[4]
    tap_count = filter_taps.shape[0]
    extended = jnp.concatenate([earlier, channels], axis=4)
    running = jnp.zeros_like(channels)
    for tap_index in range(tap_count):
        offset = tap_count - 1 - tap_index
        running = (
            running + filter_taps[tap_index][:, None] * extended[..., offset : offset + length]
        )
    channel_shape = channels.shape
    return (
        jnp.swapaxes(running, 3, 4)
        .reshape(channel_shape[0], channel_shape[1], 2, length * channel_shape[3])
        .astype(jnp.bfloat16)
    )


def on_device(voltages, pointing_table, beam_pointing, subband_order, live_subbands, filter_taps):
    local_subbands = voltages.shape[0]
    inputs = voltages.shape[2]
    local_time = voltages.shape[3]
    beam_count = beam_pointing.shape[0]
    rim_width = filter_taps.shape[0] - 1
    chosen = jnp.take(pointing_table, beam_pointing, axis=2)
    real_weight = chosen[:, 0]
    imag_weight = chosen[:, 1]
    stacked = jnp.stack(
        [
            jnp.concatenate([real_weight, -imag_weight], axis=2),
            jnp.concatenate([imag_weight, real_weight], axis=2),
        ],
        axis=2,
    )
    stacked = stacked.reshape(local_subbands, 2 * beam_count, 2 * inputs)
    signal = voltages.reshape(local_subbands, 2 * inputs, local_time)
    formed = jnp.einsum("sqi,sit->sqt", stacked, signal, preferred_element_type=jnp.float32).astype(
        jnp.bfloat16
    )
    inverse_rows = inverse_table(filter_taps.shape[1])
    axis_devices = lax.axis_size("sub")
    beam_part = beam_count // axis_devices
    blocks = formed.reshape(local_subbands, axis_devices, beam_part, 2, local_time)
    beam_rows = lax.all_to_all(blocks, "sub", split_axis=1, concat_axis=0, tiled=True)[:, 0]
    grouped, channels = spectrum_channels(beam_rows, subband_order, live_subbands, inverse_rows)
    earlier = shifted(channels[..., local_time - rim_width :].astype(jnp.bfloat16), "tm", 1).astype(
        jnp.float32
    )
    return polyphase(channels, earlier, filter_taps)


def solution(mesh):
    in_specs = (P("sub", None, None, "tm"), P("sub", None, None, None), P(), P(), P(), P())
    out_specs = P("sub", None, None, "tm")
    return jax.shard_map(
        on_device, mesh=mesh, in_specs=in_specs, out_specs=out_specs, check_vma=False
    )
```

profile of v0, /device:TPU:13, one launch (start us, length us, event | category | flops | bytes accessed | tf_op | source)
XLA Modules:
  0.0 791.4 jit_solution(15740473894358660357)
XLA Ops:
  0.0 0.7 compare_and_fusion
  0.7 0.7 compare_select_fusion
  1.4 5.8 copy.47
  7.1 5.2 gather_fusion
  12.4 2.1 fusion.51
  14.5 2.2 fusion.62
  16.7 2.8 copy.49
  19.5 1.1 bitcast_negate_fusion
  20.6 1.3 copy.48
  21.9 1.3 maximum_bitcast_fusion
  23.2 0.2 pad_maximum_fusion.1
  23.4 5.5 copy.50
  28.9 5.2 reshape.129
  34.1 8.9 %convolution_convert_fusion = bf16[12,512,1024]{2,1,0:T(8,128)(2,1)} fusion(bf16[12,512,192]{2,1,0:T(8,128)(2,1)S(1)} %reshape.129, bf16[12,192,1024]{2,1,0:T(8,128)(2,1)} %bitcast.74), kind=kOutput, calls=%fused_computation.81 | convolution fusion | flops 2422210560 | bytes 19660800 | tf_op jit(solution)/shard_map/sqi,sit->sqt/dot_general | solution.py:78
  43.1 19.0 %reshape.131 = bf16[12,16,16,2,1024]{4,3,2,1,0:T(2,128)(2,1)} reshape(bf16[12,512,1024]{2,1,0:T(8,128)(2,1)} %convolution_convert_fusion) | data formatting | bytes 25165824 | tf_op jit(solution)/shard_map/reshape | solution.py:84
  62.1 0.0 copy-start.1
  62.1 12.5 %copy.52 = bf16[12,16,16,2,1024]{4,2,3,0,1:T(8,128)(2,1)} copy(bf16[12,16,16,2,1024]{4,3,2,1,0:T(2,128)(2,1)} %reshape.131) | data formatting | bytes 25165824 | tf_op jit(solution)/shard_map/reshape | solution.py:84
  74.6 6.5 all-to-all-start
  81.8 0.0 copy-done.1
  81.8 0.1 broadcast_in_dim.41
  81.9 0.1 fusion.60
  82.0 0.1 sine_convert_fusion
  82.1 271.3 %all-to-all-done = bf16[12,16,16,2,1024]{4,2,3,0,1:T(8,128)(2,1)} async-done(((bf16[12,16,16,2,1024]{4,2,3,0,1:T(8,128)(2,1)}), bf16[12,16,16,2,1024]{4,2,3,0,1:T(8,128)(2,1)}, u32[]{:S(2)}, u32[]{:S(2)}) %all-to-all-start) | async-done | bytes 12582944 | tf_op jit(solution)/shard_map/all_to_all | solution.py:85
  353.4 12.8 %gather_fusion.1 = bf16[192,16,2,1024]{3,1,2,0:T(8,128)(2,1)} fusion(bf16[192,16,2,1024]{3,1,2,0:T(8,128)(2,1)} %bitcast.10, s32[1024]{0:T(1024)S(1)} %pad_clamp_fusion), kind=kCustom, calls=%fused_computation.1 | custom fusion | bytes 25166592 | tf_op jit(solution)/shard_map/jit(_take)/gather | solution.py:30
  366.2 6.8 select_bitcast_fusion
  372.9 0.0 copy-start
  373.0 12.4 %fusion.48 = f32[16,12,2,16,1024]{4,3,2,0,1:T(8,128)} fusion(bf16[12,16,16,2,1024,1]{4,2,3,1,0,5:T(8,128)(2,1)S(1)} %select_bitcast_fusion, bf16[1,16,2,16]{3,1,2,0:T(8,128)(2,1)S(1)} %get-tuple-element.26, bf16[1,16,2,16]{3,1,2,0:T(8,128)(2,1)S(1)} %get-tuple-element.25), kind=kOutput, calls=%fused_computation.80 | convolution fusion | flops 402657280 | bytes 37750784 | tf_op jit(solution)/shard_map/qkpc,gcbpt->bgqkt/dot_general | solution.py:36
  385.3 2.4 slice.415
  387.7 3.1 copy.54
  390.9 4.3 collective-permute-start
  395.2 0.0 copy-done
  395.2 30.3 %collective-permute-done = bf16[16,12,2,16,15]{3,0,4,2,1:T(8,128)(2,1)} collective-permute-done((bf16[16,12,2,16,15]{3,0,4,2,1:T(8,128)(2,1)S(1)}, bf16[16,12,2,16,15]{3,0,4,2,1:T(8,128)(2,1)}, u32[]{:S(2)}, u32[]{:S(2)}) %collective-permute-start) | collective-permute-done | bytes 184352 | tf_op jit(solution)/shard_map/ppermute | solution.py:12
  425.5 3.5 copy.55
  429.0 168.7 %fusion.47 = bf16[16,12,2,1024,16]{3,4,2,0,1:T(8,128)(2,1)} fusion(f32[16,12,2,16,1024]{4,3,2,0,1:T(8,128)} %fusion.48, f32[16,12,2,16,15]{4,3,2,0,1:T(8,128)S(1)} %copy.55, f32[16]{0:T(128)S(1)} %get-tuple-element.23, f32[16]{0:T(128)S(1)} %get-tuple-element.24, f32[16]{0:T(128)S(1)} %get-tuple-element.10, f32[16]{0:T(128)S(1)} %get-tuple-element.11, ...), kind=kLoop, calls=%fused_computation.79 | loop fusion | flops 295698432 | bytes 38118400 | tf_op jit(solution)/shard_map/convert_element_type | solution.py:56
  597.7 77.5 %copy.64 = bf16[16,12,2,1024,16]{4,3,2,1,0:T(8,128)(2,1)} copy(bf16[16,12,2,1024,16]{3,4,2,0,1:T(8,128)(2,1)} %fusion.47) | data formatting | bytes 25165824 | tf_op jit(solution)/shard_map/convert_element_type | solution.py:56
  675.3 116.1 %reshape.153 = bf16[16,12,2,16384]{3,2,1,0:T(2,128)(2,1)} reshape(bf16[16,12,2,1024,16]{4,3,2,1,0:T(8,128)(2,1)} %copy.64) | data formatting | bytes 25165824 | tf_op jit(solution)/shard_map/convert_element_type | solution.py:56
  (7 shorter events, 0.1 us)
Async XLA Ops:
  62.1 19.7 %copy-start.1 = (s32[192]{0:T(256)S(1)}, s32[192]{0:T(256)}, u32[]{:S(2)}) copy-start(s32[192]{0:T(256)} %param.9) | copy-start | bytes 2308
  74.6 278.8 %all-to-all-start = ((bf16[12,16,16,2,1024]{4,2,3,0,1:T(8,128)(2,1)}), bf16[12,16,16,2,1024]{4,2,3,0,1:T(8,128)(2,1)}, u32[]{:S(2)}, u32[]{:S(2)}) async-start(bf16[12,16,16,2,1024]{4,2,3,0,1:T(8,128)(2,1)} %copy.52), calls=%async_computation | async-start | bytes 25165824 | tf_op jit(solution)/shard_map/all_to_all | solution.py:85
  372.9 22.2 %copy-start = (f32[16,16]{1,0:T(8,128)S(1)}, f32[16,16]{1,0:T(8,128)}, u32[]{:S(2)}) copy-start(f32[16,16]{1,0:T(8,128)} %param.11) | copy-start | bytes 3076
  390.9 34.6 %collective-permute-start = (bf16[16,12,2,16,15]{3,0,4,2,1:T(8,128)(2,1)S(1)}, bf16[16,12,2,16,15]{3,0,4,2,1:T(8,128)(2,1)}, u32[]{:S(2)}, u32[]{:S(2)}) collective-permute-start(bf16[16,12,2,16,15]{3,0,4,2,1:T(8,128)(2,1)S(1)} %copy.54), channel_id=1, source_target_pairs={{0,1},{2,3},{4,5},{6,7},{8,9},{10,11},{12,13},{14,15},{16,17},{18,... | collective-permute-start | bytes 552968 | tf_op jit(solution)/shard_map/ppermute | solution.py:12
where the time goes:
time: 799 us; the launch traced here: 791 us
  waiting for transfers between devices  302 us (38%)
  local copies, waits for them, and re-layouts  275 us (34%)
  other arithmetic  182 us (23%)
  matrix products  21.3 us (3%)
  starting transfers between devices  10.8 us (1%)
    all_to_all x1, waiting for transfers between devices, on_device(): lax.all_to_all(blocks, 'sub', split_axis=1, concat_axis=0, tiled=True)[:, 0]  271 us
    convert_element_type x2, local copies, waits for them, and re-layouts, polyphase(): return jnp.swapaxes(running, 3, 4).reshape(channel_shape[0], channel_shap...  194 us
    convert_element_type x1, other arithmetic, polyphase(): return jnp.swapaxes(running, 3, 4).reshape(channel_shape[0], channel_shap...  169 us
    reshape x2, local copies, waits for them, and re-layouts, on_device(): formed.reshape(local_subbands, axis_devices, beam_part, 2, local_time)  31.6 us
    ppermute x1, waiting for transfers between devices, shifted(): return lax.ppermute(block, axis, route)  30.3 us
  transfers between devices with their start and end apart: 2, of which 2 were waited for; matrix products, arithmetic and copies ran while one was open for 0% of the time, Pallas kernels for 0%

commit v1 on v0

v1 whole, which is shorter than its diff:
```python
import functools
import math

import jax
import jax.numpy as jnp
from jax import lax
from jax.experimental import pallas as pl
from jax.experimental.pallas import tpu as pltpu
from jax.sharding import PartitionSpec as P

LANES = 128
CHUNKS = 4


def inverse_table(channel_count):
    channel_index = jnp.arange(channel_count, dtype=jnp.int32)
    phase = (jnp.outer(channel_index, channel_index) % channel_count).astype(jnp.float32) * (
        2.0 * math.pi / channel_count
    )
    cosine = jnp.cos(phase).astype(jnp.bfloat16)
    sine = jnp.sin(phase).astype(jnp.bfloat16)
    upper = jnp.stack([cosine, -sine], axis=0)
    lower = jnp.stack([sine, cosine], axis=0)
    return jnp.stack([upper, lower], axis=0).astype(jnp.float32)


def coefficients(filter_taps, step, shifts):
    taps, channels = filter_taps.shape
    table = inverse_table(channels)
    v = jnp.arange(step)[None, None, :]
    u = jnp.arange(step)[None, :, None]
    s = jnp.arange(shifts)[:, None, None]
    tap = v - u + step * s
    one_hot = (tap[..., None] == jnp.arange(taps)).astype(jnp.float32)
    chosen = jnp.einsum("suvj,jk->suvk", one_hot, filter_taps, precision=lax.Precision.HIGHEST)
    return jnp.einsum(
        "suvk,pqkc->cquspvk", chosen, table, precision=lax.Precision.HIGHEST
    ).reshape(channels * 2 * step, shifts * 2 * step * channels)


def form_kernel(step, table_ref, pick_ref, order_ref, volt_ref, *out_refs):
    pick = pick_ref[...]
    real = jnp.dot(pick, table_ref[0, 0], preferred_element_type=jnp.float32)
    imag = jnp.dot(pick, table_ref[0, 1], preferred_element_type=jnp.float32)
    rows = jnp.concatenate([real, -imag], axis=1).astype(jnp.bfloat16)
    cols = jnp.concatenate([imag, real], axis=1).astype(jnp.bfloat16)
    signal = jnp.dot(volt_ref[0], order_ref[...], preferred_element_type=jnp.float32)
    signal = signal.astype(jnp.bfloat16)
    part = pick.shape[0] // len(out_refs)
    for index, out_ref in enumerate(out_refs):
        mine = slice(index * part, (index + 1) * part)
        up = jnp.dot(rows[mine], signal, preferred_element_type=jnp.float32)
        low = jnp.dot(cols[mine], signal, preferred_element_type=jnp.float32)
        up = up.reshape(part, step, up.shape[1] // step)
        low = low.reshape(part, step, low.shape[1] // step)
        out_ref[0] = jnp.concatenate([up, low], axis=1).astype(jnp.bfloat16)


def synth_kernel(channels, step, shifts, order_ref, live_ref, *refs):
    slots = refs[:channels]
    coef_ref, halo_ref, out_ref = refs[channels:]
    group = pl.program_id(0)
    beams = slots[0].shape[1]
    length = slots[0].shape[3]
    width = 2 * LANES
    stacked = []
    for b in range(beams):
        pieces = []
        for c in range(channels):
            block = slots[c][0, b]
            alive = group * channels + c < live_ref[0]
            pieces.append(jnp.where(alive, block, jnp.zeros_like(block)))
        stacked.append(jnp.concatenate(pieces, axis=0).T)
    lhs = jnp.concatenate(stacked, axis=0)
    sums = jnp.dot(lhs, coef_ref[...], preferred_element_type=jnp.float32)
    row = lax.broadcasted_iota(jnp.int32, (length, width), 0)
    for b in range(beams):
        own = sums[b * length : (b + 1) * length]
        total = own[:, :width]
        for s in range(1, shifts):
            moved = pltpu.roll(own[:, s * width : (s + 1) * width], s, 0)
            total = total + jnp.where(row >= s, moved, 0.0)
        head = total[:8] + halo_ref[0, b]
        total = jnp.concatenate([head, total[8:]], axis=0)
        out_ref[b, 0] = total.reshape(2 * length, LANES).astype(jnp.bfloat16)


def on_device(voltages, pointing_table, beam_pointing, subband_order, live_subbands, filter_taps):
    local = voltages.shape[0]
    inputs = voltages.shape[2]
    time = voltages.shape[3]
    pointings = pointing_table.shape[2]
    beam_count = beam_pointing.shape[0]
    taps, channels = filter_taps.shape
    slot_count = subband_order.shape[0]
    groups = slot_count // channels
    peers = lax.axis_size("sub")
    beam_part = beam_count // peers
    chunks = CHUNKS if beam_part % CHUNKS == 0 else 1
    size = beam_part // chunks
    step = LANES // channels
    blocks = time // step
    shifts = 1 + -(-(taps - 1) // step)
    rim = step * (shifts - 1)
    rows = 2 * step

    signal = voltages.reshape(local, 2 * inputs, time)
    span = lax.axis_size("tm")
    route = [(i - 1, i) for i in range(1, span)]
    edge = lax.ppermute(signal[:, :, time - rim :], "tm", route)

    pointing = beam_pointing.reshape(peers, chunks, size).transpose(1, 0, 2).reshape(-1)
    pick = (pointing[:, None] == jnp.arange(pointings)[None, :]).astype(jnp.bfloat16)
    source = jnp.arange(time, dtype=jnp.int32)
    order = (
        source[:, None] == ((source % blocks) * step + source // blocks)[None, :]
    ).astype(jnp.bfloat16)

    part = beam_count // chunks
    formed = pl.pallas_call(
        functools.partial(form_kernel, step),
        grid=(local,),
        in_specs=[
            pl.BlockSpec((1, 2, pointings, inputs), lambda s: (s, 0, 0, 0)),
            pl.BlockSpec((beam_count, pointings), lambda s: (0, 0)),
            pl.BlockSpec((time, time), lambda s: (0, 0)),
            pl.BlockSpec((1, 2 * inputs, time), lambda s: (s, 0, 0)),
        ],
        out_specs=[pl.BlockSpec((1, part, rows, blocks), lambda s: (s, 0, 0, 0))] * chunks,
        out_shape=[jax.ShapeDtypeStruct((local, part, rows, blocks), jnp.bfloat16)] * chunks,
        compiler_params=pltpu.CompilerParams(dimension_semantics=("arbitrary",)),
        name="form",
    )(pointing_table, pick, order, signal)

    arrived = [
        lax.all_to_all(
            f.reshape(local, peers, size, rows, blocks), "sub", split_axis=1, concat_axis=0, tiled=True
        ).reshape(slot_count, size, rows, blocks)
        for f in formed
    ]

    chosen = jnp.take(pointing_table, beam_pointing, axis=2)
    weight = jnp.concatenate(
        [
            jnp.concatenate([chosen[:, 0], -chosen[:, 1]], axis=2),
            jnp.concatenate([chosen[:, 1], chosen[:, 0]], axis=2),
        ],
        axis=1,
    )
    edge_formed = jnp.einsum(
        "sqi,sit->sqt", weight, edge, preferred_element_type=jnp.float32
    ).astype(jnp.bfloat16)
    edge_formed = edge_formed.reshape(local, 2, peers, beam_part * rim).transpose(0, 2, 1, 3)
    edge_rows = lax.all_to_all(edge_formed, "sub", split_axis=1, concat_axis=0, tiled=True)
    edge_rows = jnp.take(edge_rows[:, 0], subband_order, axis=0)
    live_mask = jnp.arange(slot_count, dtype=jnp.int32) < live_subbands[0]
    edge_rows = jnp.where(live_mask[:, None, None], edge_rows, jnp.zeros_like(edge_rows))
    edge_rows = edge_rows.reshape(groups, channels, 2, beam_part, shifts - 1, step)

    wide = coefficients(filter_taps, step, shifts)
    coef = wide.astype(jnp.bfloat16)
    split = coef.reshape(channels, 2, step, shifts, 2 * LANES)
    parts = []
    for r in range(8):
        terms = jnp.zeros((groups, beam_part, 2 * LANES), jnp.float32)
        for s in range(r + 1, shifts):
            terms = terms + jnp.einsum(
                "gcqbu,cqun->gbn",
                edge_rows[:, :, :, :, shifts - 1 + r - s],
                split[:, :, :, s],
                preferred_element_type=jnp.float32,
            )
        parts.append(terms)
    halo = jnp.stack(parts, axis=2)

    results = []
    for index, block in enumerate(arrived):
        def slot_map(c):
            return lambda g, order_ref, live_ref: (order_ref[g * channels + c], 0, 0, 0)

        results.append(
            pl.pallas_call(
                functools.partial(synth_kernel, channels, step, shifts),
                grid_spec=pltpu.PrefetchScalarGridSpec(
                    num_scalar_prefetch=2,
                    grid=(groups,),
                    in_specs=[
                        pl.BlockSpec((1, size, rows, blocks), slot_map(c)) for c in range(channels)
                    ]
                    + [
                        pl.BlockSpec(coef.shape, lambda g, *_: (0, 0)),
                        pl.BlockSpec((1, size, 8, 2 * LANES), lambda g, *_: (g, index, 0, 0)),
                    ],
                    out_specs=pl.BlockSpec((size, 1, 2 * blocks, LANES), lambda g, *_: (0, g, 0, 0)),
                ),
                out_shape=jax.ShapeDtypeStruct((size, groups, 2 * blocks, LANES), jnp.bfloat16),
                compiler_params=pltpu.CompilerParams(dimension_semantics=("arbitrary",)),
                name="synth",
            )(subband_order, live_subbands, *([block] * channels), coef, halo)
        )
    out = jnp.concatenate(results, axis=0)
    out = out.reshape(beam_part, groups, blocks, 2, LANES).transpose(0, 1, 3, 2, 4)
    return out.reshape(beam_part, groups, 2, blocks * LANES)


def solution(mesh):
    in_specs = (P("sub", None, None, "tm"), P("sub", None, None, None), P(), P(), P(), P())
    out_specs = P("sub", None, None, "tm")
    return jax.shard_map(
        on_device, mesh=mesh, in_specs=in_specs, out_specs=out_specs, check_vma=False
    )
```

time: 799 us -> 396 us (0.50)
  local copies, waits for them, and re-layouts: 275 us -> 60.1 us
  other arithmetic: 182 us -> 19 us
  waiting for transfers between devices: 302 us -> 211 us
  Pallas kernels: 0 us -> 65.5 us
  starting transfers between devices: 10.8 us -> 31.1 us
  matrix products: 21.3 us -> 3.89 us
    convert_element_type x3, local copies, waits for them, and re-layouts: 197 us -> 8.61 us  [the longest x2 7.79 us: on_device(): coef = wide.astype(jnp.bfloat16)]
    convert_element_type x2 -> x4, other arithmetic: 169 us -> 3.93 us  [the longest x1 2.25 us: on_device(): order = (source[:, None] == (source % blocks * step + source // blocks)[N...]
    pallas_call x0 -> x5, Pallas kernels: none -> 65.5 us  [the longest x4 47.1 us: on_device(): pl.pallas_call(functools.partial(synth_kernel, channels, step, shifts), g...]
    all_to_all x1 -> x5, waiting for transfers between devices: 271 us -> 211 us  [the longest x4 211 us: on_device(): lax.all_to_all(f.reshape(local, peers, size, rows, blocks), 'sub', split_...]
    ppermute x1, waiting for transfers between devices: 30.3 us -> 0.01 us  [on_device(): edge = lax.ppermute(signal[:, :, time - rim:], 'tm', route)]
    all_to_all x1 -> x5, starting transfers between devices: 6.52 us -> 27.3 us  [the longest x4 20.5 us: on_device(): lax.all_to_all(f.reshape(local, peers, size, rows, blocks), 'sub', split_...]
    dot_general x2 -> x5, matrix products: 21.3 us -> 3.89 us  [the longest x3 2.35 us: on_device(): jnp.einsum('gcqbu,cqun->gbn', edge_rows[:, :, :, :, shifts - 1 + r - s],...]
    reshape x3 -> x6, local copies, waits for them, and re-layouts: 36.8 us -> 21 us  [the longest x4 18.1 us: on_device(): f.reshape(local, peers, size, rows, blocks)]
  transfers between devices with their start and end apart: 2 -> 6, of which waited for: 2 -> 4; matrix products, arithmetic and copies ran while one was open for 0% -> 16% of each run, Pallas kernels for 0% -> 14%
where the time goes in v1:
time: 396 us; the launch traced here: 391 us
  waiting for transfers between devices  211 us (53%)
  Pallas kernels  65.5 us (17%)
  local copies, waits for them, and re-layouts  60.1 us (15%)
  starting transfers between devices  31.1 us (8%)
  other arithmetic  19 us (5%)
    all_to_all x4, waiting for transfers between devices, on_device(): lax.all_to_all(f.reshape(local, peers, size, rows, blocks), 'sub', split_...  211 us
    pallas_call x4, Pallas kernels, on_device(): pl.pallas_call(functools.partial(synth_kernel, channels, step, shifts), g...  47.1 us
    all_to_all x4, starting transfers between devices, on_device(): lax.all_to_all(f.reshape(local, peers, size, rows, blocks), 'sub', split_...  20.5 us
    pallas_call x1, Pallas kernels, on_device(): pl.pallas_call(functools.partial(form_kernel, step), grid=(local,), in_sp...  18.5 us
    reshape x4, local copies, waits for them, and re-layouts, on_device(): f.reshape(local, peers, size, rows, blocks)  18.1 us
    unnamed x18, local copies, waits for them, and re-layouts  10.8 us
    gather x2, local copies, waits for them, and re-layouts, on_device(): chosen = jnp.take(pointing_table, beam_pointing, axis=2)  9.78 us
    concatenate x1, other arithmetic, on_device(): out = jnp.concatenate(results, axis=0)  9.52 us
  transfers between devices with their start and end apart: 6, of which 4 were waited for; matrix products, arithmetic and copies ran while one was open for 16% of the time, Pallas kernels for 14%

profile of v1, /device:TPU:13, one launch (start us, length us, event | category | flops | bytes accessed | tf_op | source)
XLA Modules:
  0.0 391.5 jit_solution(15543252747756135238)
XLA Ops:
  0.0 1.4 slice.36
  1.4 0.9 copy.41
  2.3 3.7 collective-permute-start
  6.1 0.7 compare_and_fusion
  6.8 0.7 compare_select_fusion
  7.4 1.4 reshape.197
  8.9 4.5 %copy.39 = bf16[12,2,320,96]{3,1,2,0:T(2,128)(2,1)} copy(bf16[12,2,320,96]{2,3,1,0:T(8,128)(2,1)S(1)} %copy-done.5) | data formatting | bytes 2949120 | tf_op args[1]
  13.3 6.8 %gather_fusion = bf16[256,12,2,96]{3,2,1,0:T(2,128)(2,1)S(1)} fusion(bf16[12,2,320,96]{3,1,2,0:T(2,128)(2,1)} %copy.39, s32[1024]{0:T(1024)S(1)} %pad_clamp_fusion.1), kind=kCustom, calls=%fused_computation | custom fusion | bytes 2360320 | tf_op jit(solution)/shard_map/jit(_take)/gather | solution.py:142
  20.1 3.0 copy.40
  23.1 1.4 select_bitcast_fusion
  24.5 0.1 slice_bitcast_fusion.5
  24.6 0.6 copy-done.6
  25.2 0.6 copy.34
  25.9 0.9 eq.24
  26.7 0.8 fusion.15.pick_ref
  27.5 2.4 copy.35.table_ref
  29.9 1.3 fusion.11
  31.2 0.8 copy.42
  32.1 1.5 reshape.201
  33.5 0.8 copy.43
  34.4 6.8 %all-to-all-start.1 = ((bf16[12,16,2,256]{3,2,0,1:T(2,128)(2,1)}), bf16[12,16,2,256]{3,2,0,1:T(2,128)(2,1)S(1)}, u32[]{:S(2)}, u32[]{:S(2)}) async-start(bf16[12,16,2,256]{3,2,0,1:T(2,128)(2,1)} %copy.43), calls=%async_computation.1 | async-start | bytes 393216 | tf_op jit(solution)/shard_map/all_to_all | solution.py:154
  41.2 2.2 fusion.order_ref
  43.4 18.5 %form.1 = (bf16[12,64,16,128]{3,2,1,0:T(8,128)(2,1)}, bf16[12,64,16,128]{3,2,1,0:T(8,128)(2,1)}, bf16[12,64,16,128]{3,2,1,0:T(8,128)(2,1)}, bf16[12,64,16,128]{3,2,1,0:T(8,128)(2,1)}) custom-call(bf16[12,2,320,96]{3,2,1,0:T(8,128)(2,1)} %copy.35.table_ref, bf16[256,320]{1,0:T(8,128)(2,1)} %fusion.15.pick_ref, bf16[1024,1024]{1,0:T(8,128)(2,1)} %fusion.order_ref, ...), custom_call_target="tpu_custom_call" | custom-call | tf_op jit(solution)/shard_map/form/pallas_call | solution.py:120
  61.9 4.5 %copy.47 = bf16[12,16,4,16,128]{4,3,2,0,1:T(8,128)(2,1)} copy(bf16[12,16,4,16,128]{4,3,2,1,0:T(8,128)(2,1)} %bitcast.140) | data formatting | bytes 6291456 | tf_op jit(solution)/shard_map/reshape | solution.py:137
  66.5 6.2 %all-to-all-start.2 = ((bf16[12,16,4,16,128]{4,3,2,0,1:T(8,128)(2,1)}), bf16[12,16,4,16,128]{4,3,2,0,1:T(8,128)(2,1)S(1)}, u32[]{:S(2)}, u32[]{:S(2)}) async-start(bf16[12,16,4,16,128]{4,3,2,0,1:T(8,128)(2,1)} %copy.47), calls=%async_computation.2 | async-start | bytes 6291456 | tf_op jit(solution)/shard_map/all_to_all | solution.py:136
  72.7 4.5 %copy.36 = bf16[12,16,4,16,128]{4,3,2,0,1:T(8,128)(2,1)} copy(bf16[12,16,4,16,128]{4,3,2,1,0:T(8,128)(2,1)} %bitcast.139) | data formatting | bytes 6291456 | tf_op jit(solution)/shard_map/reshape | solution.py:137
  77.2 65.4 %all-to-all-done.2 = bf16[12,16,4,16,128]{4,3,2,0,1:T(8,128)(2,1)S(1)} async-done(((bf16[12,16,4,16,128]{4,3,2,0,1:T(8,128)(2,1)}), bf16[12,16,4,16,128]{4,3,2,0,1:T(8,128)(2,1)S(1)}, u32[]{:S(2)}, u32[]{:S(2)}) %all-to-all-start.2) | async-done | bytes 3145760 | tf_op jit(solution)/shard_map/all_to_all | solution.py:136
  142.6 1.7 copy-done.2
  144.2 4.8 %all-to-all-start = ((bf16[12,16,4,16,128]{4,3,2,0,1:T(8,128)(2,1)}), bf16[12,16,4,16,128]{4,3,2,0,1:T(8,128)(2,1)}, u32[]{:S(2)}, u32[]{:S(2)}) async-start(bf16[12,16,4,16,128]{4,3,2,0,1:T(8,128)(2,1)} %copy.36), calls=%async_computation | async-start | bytes 6291456 | tf_op jit(solution)/shard_map/all_to_all | solution.py:136
  149.0 4.5 %copy.48 = bf16[12,16,4,16,128]{4,3,2,0,1:T(8,128)(2,1)} copy(bf16[12,16,4,16,128]{4,3,2,1,0:T(8,128)(2,1)} %bitcast.138) | data formatting | bytes 6291456 | tf_op jit(solution)/shard_map/reshape | solution.py:137
  153.5 65.5 %all-to-all-done = bf16[12,16,4,16,128]{4,3,2,0,1:T(8,128)(2,1)} async-done(((bf16[12,16,4,16,128]{4,3,2,0,1:T(8,128)(2,1)}), bf16[12,16,4,16,128]{4,3,2,0,1:T(8,128)(2,1)}, u32[]{:S(2)}, u32[]{:S(2)}) %all-to-all-start) | async-done | bytes 3145760 | tf_op jit(solution)/shard_map/all_to_all | solution.py:136
  219.0 4.8 %all-to-all-start.3 = ((bf16[12,16,4,16,128]{4,3,2,0,1:T(8,128)(2,1)}), bf16[12,16,4,16,128]{4,3,2,0,1:T(8,128)(2,1)S(1)}, u32[]{:S(2)}, u32[]{:S(2)}) async-start(bf16[12,16,4,16,128]{4,3,2,0,1:T(8,128)(2,1)} %copy.48), calls=%async_computation.3 | async-start | bytes 6291456 | tf_op jit(solution)/shard_map/all_to_all | solution.py:136
  223.8 4.5 %copy.49 = bf16[12,16,4,16,128]{4,3,2,0,1:T(8,128)(2,1)} copy(bf16[12,16,4,16,128]{4,3,2,1,0:T(8,128)(2,1)} %bitcast.137) | data formatting | bytes 6291456 | tf_op jit(solution)/shard_map/reshape | solution.py:137
  228.3 65.4 %all-to-all-done.3 = bf16[12,16,4,16,128]{4,3,2,0,1:T(8,128)(2,1)S(1)} async-done(((bf16[12,16,4,16,128]{4,3,2,0,1:T(8,128)(2,1)}), bf16[12,16,4,16,128]{4,3,2,0,1:T(8,128)(2,1)S(1)}, u32[]{:S(2)}, u32[]{:S(2)}) %all-to-all-start.3) | async-done | bytes 3145760 | tf_op jit(solution)/shard_map/all_to_all | solution.py:136
  293.7 1.7 copy-done.3
  295.3 4.8 %all-to-all-start.4 = ((bf16[12,16,4,16,128]{4,3,2,0,1:T(8,128)(2,1)}), bf16[12,16,4,16,128]{4,3,2,0,1:T(8,128)(2,1)}, u32[]{:S(2)}, u32[]{:S(2)}) async-start(bf16[12,16,4,16,128]{4,3,2,0,1:T(8,128)(2,1)} %copy.49), calls=%async_computation.4 | async-start | bytes 6291456 | tf_op jit(solution)/shard_map/all_to_all | solution.py:136
  300.1 0.1 fusion.33
  300.2 0.1 sine_convert_fusion
  300.3 0.1 copy.37
  300.4 0.1 broadcast_add_fusion
  300.5 0.2 convolution_bitcast_fusion.3
  300.7 0.8 fusion.1
  301.5 3.7 convert_element_type.79.refs_16_
  305.2 4.1 %reshape.234 = bf16[16,2,8,3,256]{4,3,2,1,0:T(4,128)(2,1)} reshape(bf16[16,2,8,3,2,8,16]{6,5,4,3,2,1,0:T(8,128)(2,1)S(1)} %fusion.1) | data formatting | bytes 786432 | tf_op jit(solution)/shard_map/convert_element_type | solution.py:161
  310.0 0.1 pad.7.clone
  310.1 0.1 pad.6.clone
  310.2 0.1 broadcast_in_dim.49
  310.3 1.9 fusion.36
  312.2 1.1 gather_fusion.1
  313.2 0.2 copy.44
  313.4 1.4 gather.12
  314.9 1.0 fusion.10
  315.9 0.8 convolution_bitcast_fusion.1
  316.7 0.8 fusion.14
  317.5 0.1 stack.39
  317.6 0.8 convolution_bitcast_fusion
  318.4 0.1 stack.40
  318.5 1.5 maximum_maximum_fusion.refs_17_
  320.1 11.7 %synth.5 = bf16[4,12,256,128]{3,2,1,0:T(8,128)(2,1)} custom-call(s32[192]{0:T(256)} %order_ref.7, s32[1]{0:T(128)} %copy.70.live_ref, bf16[192,4,16,128]{3,2,1,0:T(8,128)(2,1)} %bitcast.103, bf16[192,4,16,128]{3,2,1,0:T(8,128)(2,1)} %bitcast.104, bf16[192,4,16,128]{3,2,1,0:T(8,128)(2,1)} %bitcast.105, bf16[192,4,16,128]{3,2,1,0:T(8,128)(2,1)} %bitcast.106, ...), custom_call_target="tpu_custom_call" | custom-call | tf_op jit(solution)/shard_map/synth/pallas_call | solution.py:182
  331.8 11.7 %synth.4 = bf16[4,12,256,128]{3,2,1,0:T(8,128)(2,1)} custom-call(s32[192]{0:T(256)} %order_ref.7, s32[1]{0:T(128)} %copy.70.live_ref, bf16[192,4,16,128]{3,2,1,0:T(8,128)(2,1)} %bitcast.5.refs_0_.refs_1_.refs_2_.refs_3_.refs_4_.refs_5_.refs_6_.refs_7_.refs_8_.refs_9_.refs_10_.refs_11_.refs_12_.refs_13_.refs_14_.refs_15_, ...), custom_call_target="tpu_custom_call" | custom-call | tf_op jit(solution)/shard_map/synth/pallas_call | solution.py:182
  343.5 11.8 %synth.6 = bf16[4,12,256,128]{3,2,1,0:T(8,128)(2,1)} custom-call(s32[192]{0:T(256)} %order_ref.7, s32[1]{0:T(128)} %copy.70.live_ref, bf16[192,4,16,128]{3,2,1,0:T(8,128)(2,1)} %bitcast.119, bf16[192,4,16,128]{3,2,1,0:T(8,128)(2,1)} %bitcast.120, bf16[192,4,16,128]{3,2,1,0:T(8,128)(2,1)} %bitcast.121, bf16[192,4,16,128]{3,2,1,0:T(8,128)(2,1)} %bitcast.122, ...), custom_call_target="tpu_custom_call" | custom-call | tf_op jit(solution)/shard_map/synth/pallas_call | solution.py:182
  355.3 14.8 %all-to-all-done.4 = bf16[12,16,4,16,128]{4,3,2,0,1:T(8,128)(2,1)} async-done(((bf16[12,16,4,16,128]{4,3,2,0,1:T(8,128)(2,1)}), bf16[12,16,4,16,128]{4,3,2,0,1:T(8,128)(2,1)}, u32[]{:S(2)}, u32[]{:S(2)}) %all-to-all-start.4) | async-done | bytes 3145760 | tf_op jit(solution)/shard_map/all_to_all | solution.py:136
  370.1 11.8 %synth.7 = bf16[4,12,256,128]{3,2,1,0:T(8,128)(2,1)} custom-call(s32[192]{0:T(256)} %order_ref.7, s32[1]{0:T(128)} %copy.70.live_ref, bf16[192,4,16,128]{3,2,1,0:T(8,128)(2,1)} %bitcast.47.refs_0_.refs_1_.refs_2_.refs_3_.refs_4_.refs_5_.refs_6_.refs_7_.refs_8_.refs_9_.refs_10_.refs_11_.refs_12_.refs_13_.refs_14_.refs_15_, ...), custom_call_target="tpu_custom_call" | custom-call | tf_op jit(solution)/shard_map/synth/pallas_call | solution.py:182
  382.0 9.5 %pad_maximum_fusion = bf16[16,12,256,128]{3,2,1,0:T(8,128)(2,1)} fusion(bf16[4,12,256,128]{3,2,1,0:T(8,128)(2,1)} %synth.7, bf16[4,12,256,128]{3,2,1,0:T(8,128)(2,1)} %synth.6, bf16[4,12,256,128]{3,2,1,0:T(8,128)(2,1)S(1)} %copy-done.4, bf16[4,12,256,128]{3,2,1,0:T(8,128)(2,1)} %synth.4), kind=kLoop, calls=%fused_computation.2 | loop fusion | flops 18874368 | bytes 25165824 | tf_op jit(solution)/shard_map/concatenate | solution.py:201
  (28 shorter events, 0.1 us)
Async XLA Ops:
  0.0 300.5 %copy-start = (f32[16,16]{1,0:T(8,128)S(1)}, f32[16,16]{1,0:T(8,128)}, u32[]{:S(2)}) copy-start(f32[16,16]{1,0:T(8,128)} %param.11) | copy-start | bytes 3076
  0.0 8.9 %copy-start.5 = (bf16[12,2,320,96]{2,3,1,0:T(8,128)(2,1)S(1)}, bf16[12,2,320,96]{2,3,1,0:T(8,128)(2,1)}, u32[]{:S(2)}) copy-start(bf16[12,2,320,96]{2,3,1,0:T(8,128)(2,1)} %param.7) | copy-start | bytes 4423684
  2.3 27.6 %collective-permute-start = (bf16[12,192,16]{1,2,0:T(8,128)(2,1)}, bf16[12,192,16]{1,2,0:T(8,128)(2,1)}, u32[]{:S(2)}, u32[]{:S(2)}) collective-permute-start(bf16[12,192,16]{1,2,0:T(8,128)(2,1)} %copy.41), channel_id=1, source_target_pairs={{0,1},{2,3},{4,5},{6,7},{8,9},{10,11},{12,13},{14,15},{16,17},{18,... | collective-permute-start | bytes 221192 | tf_op jit(solution)/shard_map/ppermute | solution.py:110
  24.5 0.8 copy-start.6
  34.4 32.1 %all-to-all-start.1 = ((bf16[12,16,2,256]{3,2,0,1:T(2,128)(2,1)}), bf16[12,16,2,256]{3,2,0,1:T(2,128)(2,1)S(1)}, u32[]{:S(2)}, u32[]{:S(2)}) async-start(bf16[12,16,2,256]{3,2,0,1:T(2,128)(2,1)} %copy.43), calls=%async_computation.1 | async-start | bytes 393216 | tf_op jit(solution)/shard_map/all_to_all | solution.py:154
  66.5 76.1 %all-to-all-start.2 = ((bf16[12,16,4,16,128]{4,3,2,0,1:T(8,128)(2,1)}), bf16[12,16,4,16,128]{4,3,2,0,1:T(8,128)(2,1)S(1)}, u32[]{:S(2)}, u32[]{:S(2)}) async-start(bf16[12,16,4,16,128]{4,3,2,0,1:T(8,128)(2,1)} %copy.47), calls=%async_computation.2 | async-start | bytes 6291456 | tf_op jit(solution)/shard_map/all_to_all | solution.py:136
  142.6 1.7 copy-start.2
  144.2 74.8 %all-to-all-start = ((bf16[12,16,4,16,128]{4,3,2,0,1:T(8,128)(2,1)}), bf16[12,16,4,16,128]{4,3,2,0,1:T(8,128)(2,1)}, u32[]{:S(2)}, u32[]{:S(2)}) async-start(bf16[12,16,4,16,128]{4,3,2,0,1:T(8,128)(2,1)} %copy.36), calls=%async_computation | async-start | bytes 6291456 | tf_op jit(solution)/shard_map/all_to_all | solution.py:136
  219.0 74.7 %all-to-all-start.3 = ((bf16[12,16,4,16,128]{4,3,2,0,1:T(8,128)(2,1)}), bf16[12,16,4,16,128]{4,3,2,0,1:T(8,128)(2,1)S(1)}, u32[]{:S(2)}, u32[]{:S(2)}) async-start(bf16[12,16,4,16,128]{4,3,2,0,1:T(8,128)(2,1)} %copy.48), calls=%async_computation.3 | async-start | bytes 6291456 | tf_op jit(solution)/shard_map/all_to_all | solution.py:136
  293.7 1.7 copy-start.3
  295.3 74.8 %all-to-all-start.4 = ((bf16[12,16,4,16,128]{4,3,2,0,1:T(8,128)(2,1)}), bf16[12,16,4,16,128]{4,3,2,0,1:T(8,128)(2,1)}, u32[]{:S(2)}, u32[]{:S(2)}) async-start(bf16[12,16,4,16,128]{4,3,2,0,1:T(8,128)(2,1)} %copy.49), calls=%async_computation.4 | async-start | bytes 6291456 | tf_op jit(solution)/shard_map/all_to_all | solution.py:136
  305.2 5.0 %copy-start.7 = (s32[192]{0:T(256)S(1)}, s32[192]{0:T(256)}, u32[]{:S(2)}) copy-start(s32[192]{0:T(256)} %order_ref.7) | copy-start | bytes 2308
  370.1 11.8 %copy-start.4 = (bf16[4,12,256,128]{3,2,1,0:T(8,128)(2,1)S(1)}, bf16[4,12,256,128]{3,2,1,0:T(8,128)(2,1)}, u32[]{:S(2)}) copy-start(bf16[4,12,256,128]{3,2,1,0:T(8,128)(2,1)} %synth.5) | copy-start | bytes 9437188
  382.0 9.5 %copy-start.1 = (f32[16,16]{1,0:T(8,128)S(1)}, f32[16,16]{1,0:T(8,128)}, u32[]{:S(2)}) copy-start(f32[16,16]{1,0:T(8,128)} %param.11) | copy-start | bytes 3076
